TPU v7x, 32 devices: a whole 2x2x4 slice. The times are simulated.
32 devices in a mesh: expert: 8 (over z, y), gate: 4 (over x, core).
Axes of the slice: x: 2, y: 2, z: 4, core: 2. Of those that a mesh axis runs over, the one named last changes fastest.
Arguments:
- samples: bfloat16 [6144, 4096], P('expert', 'gate'), may hold values from -4 to 4
- gate_weight: bfloat16 [4096, 32], P('gate'), may hold values from -1 to 1
- expert_ids: int32 [6144, 2], P('expert'), may hold values from 0 to 31, all different within a row; in each aligned block of 768 rows (0 to 767, 768 to 1535, ...) at most 96 rows name the same one
- pad_mask: int32 [6144], P('expert'), may hold values 0 or 1
- up_weight: bfloat16 [32, 4096, 1024], P(('expert', 'gate')), may hold values from -0.09375 to 0.09375
- down_weight: bfloat16 [32, 1024, 1024], P(('expert', 'gate')), may hold values from -0.1875 to 0.1875
Outputs:
- combined: bfloat16 [6144, 1024], P('expert', 'gate')
Inputs may be any that keep to these rules, and one draw needn't show every extreme that they name: `expert_ids`: each sample names two different experts; among the 768 samples of one index of expert no expert is named more than 96 times, a bound that some block reaches.
All inputs are finite; a program needn't handle non-finite values. No bound on the sum of `pad_mask` on one device may be relied on, other than what follows from the above.
Results may differ from a plain program's by a relative error of at most 0.0057.
Values may be sent and summed in bfloat16 or wider, within the bound.
A program may use at most 128 MiB of HBM per device.

v0:
```python
import jax
import jax.numpy as jnp
from jax import lax
from jax.sharding import PartitionSpec as P


def joined(shard, axis, combine):
    everything = jax.tree.map(lambda part: lax.all_gather(part, axis), shard)
    leading = jax.tree.map(lambda part: part[0], everything)

    def step(k, so_far):
        return combine(so_far, jax.tree.map(lambda part: part[k], everything))

    return lax.fori_loop(1, lax.axis_size(axis), step, leading)


def combine_parts(first, second):
    row_top = jnp.maximum(first[0], second[0])
    left_scale = jnp.exp(first[0] - row_top)
    right_scale = jnp.exp(second[0] - row_top)
    row_total = first[1] * left_scale + second[1] * right_scale
    chosen = first[2] * left_scale[None, :] + second[2] * right_scale[None, :]
    return (row_top, row_total, chosen)


def per_device(samples, gate_weight, expert_ids, pad_mask, up_weight, down_weight):
    row_count = samples.shape[0]
    group_count = lax.axis_size("expert")
    gate_count = lax.axis_size("gate")
    expert_count = group_count * gate_count
    capacity = 4 * row_count // expert_count
    col_count = expert_count // gate_count
    gate_index = lax.axis_index("gate")
    logits_t = lax.psum_scatter(
        lax.dot_general(
            gate_weight, samples, (((0,), (1,)), ((), ())), preferred_element_type=jnp.float32
        ),
        "gate",
        scatter_dimension=0,
        tiled=True,
    )
    flat_ids = expert_ids.reshape(-1)
    onehot = (flat_ids[:, None] == jnp.arange(expert_count, dtype=jnp.int32)[None, :]).astype(
        jnp.int32
    )
    slot_rank = jnp.sum(onehot * (jnp.cumsum(onehot, axis=0) - 1), axis=1)
    position = flat_ids * capacity + slot_rank
    row_index = jnp.repeat(jnp.arange(row_count, dtype=jnp.int32), 2)
    owners = jnp.full((expert_count * capacity,), row_count, jnp.int32).at[position].set(row_index)
    whole_rows = lax.all_gather(samples, "gate", axis=1, tiled=True)
    padded = jnp.concatenate(
        [whole_rows, jnp.zeros((1, whole_rows.shape[1]), whole_rows.dtype)], axis=0
    )
    column_owners = lax.dynamic_index_in_dim(
        owners.reshape(group_count, gate_count, capacity), gate_index, 1, keepdims=False
    )
    outgoing = padded[column_owners]
    incoming = lax.all_to_all(outgoing, "expert", split_axis=0, concat_axis=0, tiled=True)
    slot_rows = incoming.reshape(group_count * capacity, whole_rows.shape[1])
    hidden = jnp.dot(slot_rows, up_weight[0], preferred_element_type=jnp.float32)
    active = jnp.maximum(hidden, 0.0).astype(jnp.bfloat16)
    expert_out = jnp.dot(active, down_weight[0], preferred_element_type=jnp.float32).astype(
        jnp.bfloat16
    )
    out_share = expert_out.shape[1] // gate_count
    outbound = expert_out.reshape(group_count, 1, 1, capacity, gate_count, out_share)
    returned = lax.all_to_all(
        lax.all_to_all(outbound, "expert", split_axis=0, concat_axis=1, tiled=True),
        "gate",
        split_axis=4,
        concat_axis=2,
        tiled=True,
    )
    returned = returned.reshape(expert_count * capacity, out_share)
    offset = expert_ids - gate_index * col_count
    inside = ((offset >= 0) & (offset < col_count)).T
    chosen = jnp.take_along_axis(logits_t, jnp.clip(offset, 0, col_count - 1).T, axis=0)
    local_top = jnp.max(logits_t, axis=0)
    local_total = jnp.sum(jnp.exp(logits_t - local_top[None, :]), axis=0)
    local_chosen = jnp.where(inside, jnp.exp(chosen - local_top[None, :]), 0.0)
    row_top, row_total, numerator = joined(
        (local_top, local_total, local_chosen), "gate", combine_parts
    )
    factor = expert_count * numerator / row_total[None, :] * pad_mask.astype(jnp.float32)[None, :]
    picked = returned[position].astype(jnp.float32).reshape(row_count, 2, out_share)
    mixed = factor[0][:, None] * picked[:, 0, :] + factor[1][:, None] * picked[:, 1, :]
    return mixed.astype(jnp.bfloat16)


def solution(mesh):
    placed = (
        P("expert", "gate"),
        P("gate", None),
        P("expert", None),
        P("expert"),
        P(("expert", "gate"), None, None),
        P(("expert", "gate"), None, None),
    )
    return jax.shard_map(
        per_device, mesh=mesh, in_specs=placed, out_specs=P("expert", "gate"), check_vma=False
    )
```

profile of v0, /device:TPU:0, one launch (start us, length us, event | category | flops | bytes accessed | tf_op | source)
XLA Modules:
  0.0 345.1 jit_solution(15891063067835120710)
XLA Ops:
  6.5 0.7 all-gather.8.cloned.1.call-update
  7.3 0.9 copy.19
  8.1 0.2 eq.29
  8.6 0.7 broadcast_multiply_fusion
  9.5 0.3 mul.137
  9.8 9.1 %reduce-window.6 = s32[32,12,128]{2,1,0:T(8,128)S(1)} reduce-window(s32[32,12,128]{2,1,0:T(8,128)S(1)} %fusion.14, s32[]{:T(128)} %constant.77.clone.1), window={size=1x1x128 pad=0_0x0_0x127_0}, to_apply=%region_5.6 | reduce-window | flops 6242304 | bytes 393220 | tf_op jit(solution)/shard_map/reduce-window
  19.3 0.2 reshape.149
  19.8 6.2 %scatter_custom_fusion = s32[3072]{0:T(1024)S(1)} fusion(s32[1536]{0:T(1024)S(1)} %fusion.17, s32[1536]{0:T(1024)S(1)} %reshape.149, s32[]{:T(128)} %constant.86.clone.1), kind=kCustom, calls=%fused_computation.44 | custom fusion | bytes 12292 | tf_op jit(solution)/shard_map/scatter | solution.py:49
  26.2 31.8 %all-gather.8.cloned.1.call-done = bf16[768,4096]{1,0:T(8,128)(2,1)} async-done(((bf16[768,1024]{1,0:T(8,128)(2,1)}), bf16[768,4096]{1,0:T(8,128)(2,1)}) %all-gather.8.cloned.1.call-update) | async-done | bytes 6291472 | tf_op jit(solution)/shard_map/all_gather | solution.py:50
  58.0 6.2 %concatenate.3 = bf16[769,4096]{1,0:T(8,128)(2,1)} pad(bf16[768,4096]{1,0:T(8,128)(2,1)} %all-gather.8.cloned.1.call-done, bf16[]{:T(256)} %constant.85.clone.1), padding=0_1x0_0 | pad | bytes 12591106 | tf_op jit(solution)/shard_map/concatenate | solution.py:51
  64.3 15.6 %gather_fusion = bf16[768,4096]{1,0:T(8,128)(2,1)} fusion(bf16[769,4096]{1,0:T(8,128)(2,1)} %concatenate.3, s32[1024]{0:T(1024)S(1)} %pad_clamp_fusion.1), kind=kCustom, calls=%fused_computation | custom fusion | bytes 12585984 | tf_op jit(solution)/shard_map/gather | solution.py:57
  79.8 144.1 %all_to_all.32 = bf16[8,96,4096]{2,1,0:T(8,128)(2,1)} all-to-all(bf16[8,96,4096]{2,1,0:T(8,128)(2,1)} %bitcast.93), channel_id=1, replica_groups=mesh['expert'=8,'gate'=4] {'expert'}, dimensions={0} | all-to-all | bytes 12582912 | tf_op jit(solution)/shard_map/all_to_all | solution.py:58
  224.0 14.6 %fusion.7 = bf16[768,1024]{1,0:T(8,128)(2,1)} fusion(bf16[1,1024,1024]{2,1,0:T(8,128)(2,1)S(1)} %copy-done, bf16[768,4096]{1,0:T(8,128)(2,1)} %bitcast.94, bf16[1,4096,1024]{2,1,0:T(8,128)(2,1)} %param.12), kind=kOutput, calls=%fused_computation.16 | convolution fusion | flops 8055422976 | bytes 18350080 | tf_op jit(solution)/shard_map/dot_general | solution.py:62
  238.6 3.9 %reshape.120 = bf16[8,1,1,96,4,256]{5,4,3,0,2,1:T(4,128)(2,1)} reshape(bf16[768,1024]{1,0:T(8,128)(2,1)} %fusion.7) | data formatting | bytes 3145728 | tf_op jit(solution)/shard_map/reshape | solution.py:66
  242.5 4.4 %all-to-all-start.1 = ((bf16[8,1,1,96,4,256]{5,4,3,2,1,0:T(4,128)(2,1)}), bf16[8,1,1,96,4,256]{5,4,3,2,1,0:T(4,128)(2,1)}, u32[]{:S(2)}, u32[]{:S(2)}) async-start(bf16[8,1,1,96,4,256]{5,4,3,2,1,0:T(4,128)(2,1)} %bitcast.95), calls=%async_computation.2 | async-start | bytes 3145728 | tf_op jit(solution)/shard_map/all_to_all | solution.py:68
  247.0 2.6 fusion.23
  249.7 20.5 %reduce-scatter.2.cloned.1.call-done = f32[8,768]{1,0:T(8,128)} async-done(((f32[32,768]{1,0:T(8,128)}), f32[8,768]{1,0:T(8,128)}) %reduce-scatter.2.cloned.1.call-update) | async-done | bytes 24592 | tf_op jit(solution)/shard_map/reduce_scatter | solution.py:34
  270.2 0.8 reduce_max.9
  271.0 0.8 exponential_reduce_fusion
  271.8 9.4 %gather_fusion.2 = f32[1536]{0:T(1024)S(1)} fusion(f32[8,768]{1,0:T(8,128)S(1)} %copy-done.1, s32[1536]{0:T(1024)S(1)} %reshape.139), kind=kCustom, calls=%fused_computation.2 | custom fusion | bytes 24576 | tf_op jit(solution)/shard_map/jit(take_along_axis)/gather | solution.py:77
  281.2 5.2 %all-gather.3 = f32[4,1,768]{2,1,0:T(1,128)S(1)} all-gather(f32[1,1,768]{2,1,0:T(1,128)S(1)} %reshape.168), channel_id=2, replica_groups=mesh['expert'=8,'gate'=4] {'gate'}, dimensions={0}, use_global_device_ids=true | all-gather | bytes 15360 | tf_op jit(solution)/shard_map/all_gather | solution.py:8
  286.4 5.2 %all-gather.4 = f32[4,1,768]{2,1,0:T(1,128)S(1)} all-gather(f32[1,1,768]{2,1,0:T(1,128)S(1)} %reshape.170), channel_id=3, replica_groups=mesh['expert'=8,'gate'=4] {'gate'}, dimensions={0}, use_global_device_ids=true | all-gather | bytes 15360 | tf_op jit(solution)/shard_map/all_gather | solution.py:8
  291.6 5.2 %all-gather.5 = f32[4,2,768]{2,1,0:T(2,128)S(1)} all-gather(f32[1,2,768]{2,1,0:T(2,128)S(1)} %fusion.19), channel_id=4, replica_groups=mesh['expert'=8,'gate'=4] {'gate'}, dimensions={0}, use_global_device_ids=true | all-gather | bytes 30720 | tf_op jit(solution)/shard_map/all_gather | solution.py:8
  296.8 2.8 copy.24
  299.7 4.3 %all-to-all-start.2 = ((bf16[1,8,1,96,4,256]{5,3,1,2,0,4:T(8,128)(2,1)}), bf16[1,8,1,96,4,256]{5,3,1,2,0,4:T(8,128)(2,1)}, u32[]{:S(2)}, u32[]{:S(2)}) async-start(bf16[1,8,1,96,4,256]{5,3,1,2,0,4:T(8,128)(2,1)} %copy.24), calls=%async_computation.3 | async-start | bytes 3145728 | tf_op jit(solution)/shard_map/all_to_all | solution.py:67
  304.0 0.3 while.19
  304.4 19.8 %all-to-all-done.2 = bf16[1,8,1,96,4,256]{5,3,1,2,0,4:T(8,128)(2,1)} async-done(((bf16[1,8,1,96,4,256]{5,3,1,2,0,4:T(8,128)(2,1)}), bf16[1,8,1,96,4,256]{5,3,1,2,0,4:T(8,128)(2,1)}, u32[]{:S(2)}, u32[]{:S(2)}) %all-to-all-start.2) | async-done | bytes 1572896 | tf_op jit(solution)/shard_map/all_to_all | solution.py:67
  324.1 2.7 copy.25
  326.8 5.3 %gather_fusion.1 = bf16[1536,256]{1,0:T(8,128)(2,1)S(1)} fusion(bf16[3072,256]{1,0:T(8,128)(2,1)} %bitcast.92, s32[2048]{0:T(1024)S(1)} %pad_clamp_fusion), kind=kCustom, calls=%fused_computation.1 | custom fusion | bytes 1579008 | tf_op jit(solution)/shard_map/gather | solution.py:85
  332.1 1.9 reshape.122
  334.0 3.3 fusion.22
  337.2 1.0 fusion.12
  (54 shorter events, 1.7 us)
Async XLA Ops:
  6.5 217.4 %copy-start = (bf16[1,1024,1024]{2,1,0:T(8,128)(2,1)S(1)}, bf16[1,1024,1024]{2,1,0:T(8,128)(2,1)}, u32[]{:S(2)}) copy-start(bf16[1,1024,1024]{2,1,0:T(8,128)(2,1)} %param.13) | copy-start | bytes 6291460
  6.5 51.5 %all-gather.8.cloned.1.call-start = ((), (), s32[]{:S(2)}) async-start(), calls=%async_computation.5 | async-start | bytes 7864320 | tf_op jit(solution)/shard_map/all_gather | solution.py:50
  238.6 8.4 %copy-start.3 = (bf16[1024,32]{0,1:T(8,128)(2,1)S(1)}, bf16[1024,32]{0,1:T(8,128)(2,1)}, u32[]{:S(2)}) copy-start(bf16[1024,32]{0,1:T(8,128)(2,1)} %param.9) | copy-start | bytes 196612
  242.5 7.1 %copy-start.2 = (s32[768,2]{0,1:T(2,128)S(1)}, s32[768,2]{0,1:T(2,128)}, u32[]{:S(2)}) copy-start(s32[768,2]{0,1:T(2,128)} %param.10) | copy-start | bytes 18436
  242.5 7.2 %copy-start.4 = (s32[768]{0:T(1024)S(1)}, s32[768]{0:T(1024)}, u32[]{:S(2)}) copy-start(s32[768]{0:T(1024)} %param.11) | copy-start | bytes 9220
  242.5 54.3 %all-to-all-start.1 = ((bf16[8,1,1,96,4,256]{5,4,3,2,1,0:T(4,128)(2,1)}), bf16[8,1,1,96,4,256]{5,4,3,2,1,0:T(4,128)(2,1)}, u32[]{:S(2)}, u32[]{:S(2)}) async-start(bf16[8,1,1,96,4,256]{5,4,3,2,1,0:T(4,128)(2,1)} %bitcast.95), calls=%async_computation.2 | async-start | bytes 3145728 | tf_op jit(solution)/shard_map/all_to_all | solution.py:68
  246.9 23.3 %reduce-scatter.2.cloned.1.call-start = ((), (), s32[]{:S(2)}) async-start(), calls=%async_computation.4 | async-start | bytes 122880 | tf_op jit(solution)/shard_map/reduce_scatter | solution.py:34
  270.2 1.6 copy-start.1
  299.7 24.5 %all-to-all-start.2 = ((bf16[1,8,1,96,4,256]{5,3,1,2,0,4:T(8,128)(2,1)}), bf16[1,8,1,96,4,256]{5,3,1,2,0,4:T(8,128)(2,1)}, u32[]{:S(2)}, u32[]{:S(2)}) async-start(bf16[1,8,1,96,4,256]{5,3,1,2,0,4:T(8,128)(2,1)} %copy.24), calls=%async_computation.3 | async-start | bytes 3145728 | tf_op jit(solution)/shard_map/all_to_all | solution.py:67
Sparse Core Ops, SparseCore 0:
  8.9 49.0 all-gather.7
  250.1 19.9 reduce-scatter.1
where the time goes:
time: 346 us; the launch traced here: 345 us
  blocking collectives  160 us (46%)
  waiting for transfers between devices  72.8 us (21%)
  local copies, waits for them, and re-layouts  60 us (17%)
  matrix products  17.2 us (5%)
  between operations  13.7 us (4%)
  other arithmetic  12.8 us (4%)
  starting transfers between devices  8.8 us (3%)
    all_to_all x1, blocking collectives, per_device(): lax.all_to_all(outgoing, 'expert', split_axis=0, concat_axis=0, tiled=True)  144 us
    all_gather x1, waiting for transfers between devices, per_device(): whole_rows = lax.all_gather(samples, 'gate', axis=1, tiled=True)  31.8 us
    reduce_scatter x1, waiting for transfers between devices, per_device(): lax.psum_scatter(lax.dot_general(gate_weight, samples, (((0,), (1,)), (()...  20.5 us
    all_to_all x1, waiting for transfers between devices, per_device(): lax.all_to_all(lax.all_to_all(outbound, 'expert', split_axis=0, concat_ax...  19.8 us
    all_gather x3, blocking collectives, joined(): everything = jax.tree.map(lambda part: lax.all_gather(part, axis), shard)  15.6 us
    gather x1, local copies, waits for them, and re-layouts, per_device(): outgoing = padded[column_owners]  15.6 us
    dot_general x1, matrix products, per_device(): jnp.dot(active, down_weight[0], preferred_element_type=jnp.float32)  14.6 us
    gather x3, local copies, waits for them, and re-layouts, per_device(): jnp.take_along_axis(logits_t, jnp.clip(offset, 0, col_count - 1).T, axis=0)  9.39 us
  transfers between devices with their start and end apart: 4, of which 3 were waited for; matrix products, arithmetic and copies ran while one was open for 9% of the time, Pallas kernels for 0%

commit v1 on v0

--- a/solution.py
+++ b/solution.py
@@ -47,7 +47,7 @@
     position = flat_ids * capacity + slot_rank
     row_index = jnp.repeat(jnp.arange(row_count, dtype=jnp.int32), 2)
     owners = jnp.full((expert_count * capacity,), row_count, jnp.int32).at[position].set(row_index)
-    whole_rows = lax.all_gather(samples, "gate", axis=1, tiled=True)
+    whole_rows = jnp.concatenate(lax.all_gather(samples, "gate"), axis=1)
     padded = jnp.concatenate(
         [whole_rows, jnp.zeros((1, whole_rows.shape[1]), whole_rows.dtype)], axis=0
     )

time: 346 us -> 360 us (1.040)
  local copies, waits for them, and re-layouts: 60 us -> 74.4 us
    all_gather x0 -> x1, local copies, waits for them, and re-layouts: none -> 10.3 us  [per_device(): whole_rows = jnp.concatenate(lax.all_gather(samples, 'gate'), axis=1)]
    unnamed x15 -> x16, local copies, waits for them, and re-layouts: 0.9 us -> 7.79 us
where the time goes in v1:
time: 360 us; the launch traced here: 359 us
  blocking collectives  160 us (44%)
  local copies, waits for them, and re-layouts  74.4 us (21%)
  waiting for transfers between devices  72.3 us (20%)
  matrix products  17.2 us (5%)
  between operations  13.7 us (4%)
  other arithmetic  12.8 us (4%)
  starting transfers between devices  9.06 us (3%)
    all_to_all x1, blocking collectives, per_device(): lax.all_to_all(outgoing, 'expert', split_axis=0, concat_axis=0, tiled=True)  144 us
    all_gather x1, waiting for transfers between devices, per_device(): whole_rows = jnp.concatenate(lax.all_gather(samples, 'gate'), axis=1)  31.6 us
    reduce_scatter x1, waiting for transfers between devices, per_device(): lax.psum_scatter(lax.dot_general(gate_weight, samples, (((0,), (1,)), (()...  20.5 us
    all_to_all x1, waiting for transfers between devices, per_device(): lax.all_to_all(lax.all_to_all(outbound, 'expert', split_axis=0, concat_ax...  19.5 us
    gather x1, local copies, waits for them, and re-layouts, per_device(): outgoing = padded[column_owners]  15.8 us
    all_gather x3, blocking collectives, joined(): everything = jax.tree.map(lambda part: lax.all_gather(part, axis), shard)  15.6 us
    dot_general x1, matrix products, per_device(): jnp.dot(active, down_weight[0], preferred_element_type=jnp.float32)  14.6 us
    all_gather x1, local copies, waits for them, and re-layouts, per_device(): whole_rows = jnp.concatenate(lax.all_gather(samples, 'gate'), axis=1)  10.3 us
  transfers between devices with their start and end apart: 4, of which 3 were waited for; matrix products, arithmetic and copies ran while one was open for 9% of the time, Pallas kernels for 0%

profile of v1, /device:TPU:0, one launch (start us, length us, event | category | flops | bytes accessed | tf_op | source)
XLA Modules:
  0.0 359.3 jit_solution(8279300484511642544)
XLA Ops:
  6.5 0.7 all-gather.9.cloned.1.call-update
  7.3 0.9 copy.22
  8.6 0.7 broadcast_multiply_fusion
  9.5 0.3 mul.137
  9.8 9.1 %reduce-window.6 = s32[32,12,128]{2,1,0:T(8,128)S(1)} reduce-window(s32[32,12,128]{2,1,0:T(8,128)S(1)} %fusion.14, s32[]{:T(128)} %constant.77.clone.1), window={size=1x1x128 pad=0_0x0_0x127_0}, to_apply=%region_5.6 | reduce-window | flops 6242304 | bytes 393220 | tf_op jit(solution)/shard_map/reduce-window
  19.8 6.4 %scatter_custom_fusion = s32[3072]{0:T(1024)S(1)} fusion(s32[1536]{0:T(1024)S(1)} %fusion.17, s32[1536]{0:T(1024)S(1)} %reshape.157, s32[]{:T(128)} %constant.86.clone.1), kind=kCustom, calls=%fused_computation.44 | custom fusion | bytes 12292 | tf_op jit(solution)/shard_map/scatter | solution.py:49
  26.4 31.6 %all-gather.9.cloned.1.call-done = bf16[3072,1024]{1,0:T(8,128)(2,1)} async-done(((bf16[768,1024]{1,0:T(8,128)(2,1)}), bf16[3072,1024]{1,0:T(8,128)(2,1)}) %all-gather.9.cloned.1.call-update) | async-done | bytes 6291472 | tf_op jit(solution)/shard_map/all_gather | solution.py:50
  58.0 10.3 %copy.20 = bf16[4,768,1024]{2,0,1:T(4,128)(2,1)} copy(bf16[4,768,1024]{2,1,0:T(8,128)(2,1)} %bitcast.100) | data formatting | bytes 12582912 | tf_op jit(solution)/shard_map/all_gather | solution.py:50
  68.3 6.9 %copy.35 = bf16[96,8,4,1024]{3,1,2,0:T(8,128)(2,1)S(1)} copy(bf16[96,8,4,1024]{3,2,1,0:T(4,128)(2,1)} %bitcast.99) | data formatting | bytes 12582912
  75.2 3.1 concatenate.3
  78.3 15.8 %gather_fusion = bf16[768,4096]{1,0:T(8,128)(2,1)} fusion(bf16[769,4096]{1,0:T(8,128)(2,1)} %concatenate.3, s32[1024]{0:T(1024)S(1)} %pad_clamp_fusion.1), kind=kCustom, calls=%fused_computation | custom fusion | bytes 12585984 | tf_op jit(solution)/shard_map/gather | solution.py:57
  94.1 144.1 %all_to_all.32 = bf16[8,96,4096]{2,1,0:T(8,128)(2,1)} all-to-all(bf16[8,96,4096]{2,1,0:T(8,128)(2,1)} %bitcast.98), channel_id=1, replica_groups=mesh['expert'=8,'gate'=4] {'expert'}, dimensions={0} | all-to-all | bytes 12582912 | tf_op jit(solution)/shard_map/all_to_all | solution.py:58
  238.2 14.6 %fusion.7 = bf16[768,1024]{1,0:T(8,128)(2,1)} fusion(bf16[1,1024,1024]{2,1,0:T(8,128)(2,1)S(1)} %copy-done, bf16[768,4096]{1,0:T(8,128)(2,1)} %bitcast.101, bf16[1,4096,1024]{2,1,0:T(8,128)(2,1)} %param.12), kind=kOutput, calls=%fused_computation.16 | convolution fusion | flops 8055422976 | bytes 18350080 | tf_op jit(solution)/shard_map/dot_general | solution.py:62
  252.8 3.9 %reshape.128 = bf16[8,1,1,96,4,256]{5,4,3,0,2,1:T(4,128)(2,1)} reshape(bf16[768,1024]{1,0:T(8,128)(2,1)} %fusion.7) | data formatting | bytes 3145728 | tf_op jit(solution)/shard_map/reshape | solution.py:66
  256.7 4.4 %all-to-all-start.1 = ((bf16[8,1,1,96,4,256]{5,4,3,2,1,0:T(4,128)(2,1)}), bf16[8,1,1,96,4,256]{5,4,3,2,1,0:T(4,128)(2,1)}, u32[]{:S(2)}, u32[]{:S(2)}) async-start(bf16[8,1,1,96,4,256]{5,4,3,2,1,0:T(4,128)(2,1)} %bitcast.102), calls=%async_computation.2 | async-start | bytes 3145728 | tf_op jit(solution)/shard_map/all_to_all | solution.py:68
  261.2 2.6 fusion.23
  264.0 20.5 %reduce-scatter.2.cloned.1.call-done = f32[8,768]{1,0:T(8,128)} async-done(((f32[32,768]{1,0:T(8,128)}), f32[8,768]{1,0:T(8,128)}) %reduce-scatter.2.cloned.1.call-update) | async-done | bytes 24592 | tf_op jit(solution)/shard_map/reduce_scatter | solution.py:34
  284.4 0.8 reduce_max.9
  285.2 0.8 exponential_reduce_fusion
  286.0 9.4 %gather_fusion.2 = f32[1536]{0:T(1024)S(1)} fusion(f32[8,768]{1,0:T(8,128)S(1)} %copy-done.1, s32[1536]{0:T(1024)S(1)} %reshape.147), kind=kCustom, calls=%fused_computation.2 | custom fusion | bytes 24576 | tf_op jit(solution)/shard_map/jit(take_along_axis)/gather | solution.py:77
  295.4 5.2 %all-gather.4 = f32[4,1,768]{2,1,0:T(1,128)S(1)} all-gather(f32[1,1,768]{2,1,0:T(1,128)S(1)} %reshape.177), channel_id=2, replica_groups=mesh['expert'=8,'gate'=4] {'gate'}, dimensions={0}, use_global_device_ids=true | all-gather | bytes 15360 | tf_op jit(solution)/shard_map/all_gather | solution.py:8
  300.6 5.2 %all-gather.5 = f32[4,1,768]{2,1,0:T(1,128)S(1)} all-gather(f32[1,1,768]{2,1,0:T(1,128)S(1)} %reshape.179), channel_id=3, replica_groups=mesh['expert'=8,'gate'=4] {'gate'}, dimensions={0}, use_global_device_ids=true | all-gather | bytes 15360 | tf_op jit(solution)/shard_map/all_gather | solution.py:8
  305.8 5.2 %all-gather.6 = f32[4,2,768]{2,1,0:T(2,128)S(1)} all-gather(f32[1,2,768]{2,1,0:T(2,128)S(1)} %fusion.19), channel_id=4, replica_groups=mesh['expert'=8,'gate'=4] {'gate'}, dimensions={0}, use_global_device_ids=true | all-gather | bytes 30720 | tf_op jit(solution)/shard_map/all_gather | solution.py:8
  311.1 2.8 copy.27
  313.9 4.6 %all-to-all-start.2 = ((bf16[1,8,1,96,4,256]{5,3,1,2,0,4:T(8,128)(2,1)}), bf16[1,8,1,96,4,256]{5,3,1,2,0,4:T(8,128)(2,1)}, u32[]{:S(2)}, u32[]{:S(2)}) async-start(bf16[1,8,1,96,4,256]{5,3,1,2,0,4:T(8,128)(2,1)} %copy.27), calls=%async_computation.3 | async-start | bytes 3145728 | tf_op jit(solution)/shard_map/all_to_all | solution.py:67
  318.5 0.3 while.19
  318.9 19.5 %all-to-all-done.2 = bf16[1,8,1,96,4,256]{5,3,1,2,0,4:T(8,128)(2,1)} async-done(((bf16[1,8,1,96,4,256]{5,3,1,2,0,4:T(8,128)(2,1)}), bf16[1,8,1,96,4,256]{5,3,1,2,0,4:T(8,128)(2,1)}, u32[]{:S(2)}, u32[]{:S(2)}) %all-to-all-start.2) | async-done | bytes 1572896 | tf_op jit(solution)/shard_map/all_to_all | solution.py:67
  338.4 2.7 copy.28
  341.0 5.3 %gather_fusion.1 = bf16[1536,256]{1,0:T(8,128)(2,1)S(1)} fusion(bf16[3072,256]{1,0:T(8,128)(2,1)} %bitcast.96, s32[2048]{0:T(1024)S(1)} %pad_clamp_fusion), kind=kCustom, calls=%fused_computation.1 | custom fusion | bytes 1579008 | tf_op jit(solution)/shard_map/gather | solution.py:85
  346.3 1.9 reshape.130
  348.2 3.3 fusion.22
  351.5 1.0 fusion.12
  (56 shorter events, 2.2 us)
Async XLA Ops:
  6.5 231.7 %copy-start = (bf16[1,1024,1024]{2,1,0:T(8,128)(2,1)S(1)}, bf16[1,1024,1024]{2,1,0:T(8,128)(2,1)}, u32[]{:S(2)}) copy-start(bf16[1,1024,1024]{2,1,0:T(8,128)(2,1)} %param.13) | copy-start | bytes 6291460
  6.5 51.5 %all-gather.9.cloned.1.call-start = ((), (), s32[]{:S(2)}) async-start(), calls=%async_computation.5 | async-start | bytes 7864320 | tf_op jit(solution)/shard_map/all_gather | solution.py:50
  252.8 8.4 %copy-start.3 = (bf16[1024,32]{0,1:T(8,128)(2,1)S(1)}, bf16[1024,32]{0,1:T(8,128)(2,1)}, u32[]{:S(2)}) copy-start(bf16[1024,32]{0,1:T(8,128)(2,1)} %param.9) | copy-start | bytes 196612
  256.7 7.1 %copy-start.2 = (s32[768,2]{0,1:T(2,128)S(1)}, s32[768,2]{0,1:T(2,128)}, u32[]{:S(2)}) copy-start(s32[768,2]{0,1:T(2,128)} %param.10) | copy-start | bytes 18436
  256.7 7.2 %copy-start.4 = (s32[768]{0:T(1024)S(1)}, s32[768]{0:T(1024)}, u32[]{:S(2)}) copy-start(s32[768]{0:T(1024)} %param.11) | copy-start | bytes 9220
  256.7 54.3 %all-to-all-start.1 = ((bf16[8,1,1,96,4,256]{5,4,3,2,1,0:T(4,128)(2,1)}), bf16[8,1,1,96,4,256]{5,4,3,2,1,0:T(4,128)(2,1)}, u32[]{:S(2)}, u32[]{:S(2)}) async-start(bf16[8,1,1,96,4,256]{5,4,3,2,1,0:T(4,128)(2,1)} %bitcast.102), calls=%async_computation.2 | async-start | bytes 3145728 | tf_op jit(solution)/shard_map/all_to_all | solution.py:68
  261.2 23.3 %reduce-scatter.2.cloned.1.call-start = ((), (), s32[]{:S(2)}) async-start(), calls=%async_computation.4 | async-start | bytes 122880 | tf_op jit(solution)/shard_map/reduce_scatter | solution.py:34
  284.4 1.6 copy-start.1
  313.9 24.5 %all-to-all-start.2 = ((bf16[1,8,1,96,4,256]{5,3,1,2,0,4:T(8,128)(2,1)}), bf16[1,8,1,96,4,256]{5,3,1,2,0,4:T(8,128)(2,1)}, u32[]{:S(2)}, u32[]{:S(2)}) async-start(bf16[1,8,1,96,4,256]{5,3,1,2,0,4:T(8,128)(2,1)} %copy.27), calls=%async_computation.3 | async-start | bytes 3145728 | tf_op jit(solution)/shard_map/all_to_all | solution.py:67
Sparse Core Ops, SparseCore 0:
  8.9 49.0 all-gather.8
  264.4 19.9 reduce-scatter.1
